TPU v7x, 32 devices: a whole 2x2x4 slice. The times are simulated.
32 devices in a mesh: corpus: 16 (over z, y, x), dim: 2 (over core).
Axes of the slice: x: 2, y: 2, z: 4, core: 2. Of those that a mesh axis runs over, the one named last changes fastest.
Arguments:
- queries: bfloat16 [128, 768], P('dim'), as said below
- corpus: bfloat16 [8192, 768], P('corpus', 'dim'), as said below
- candidates: int32 [128, 1024], P('dim'), may hold values from 0 to 8191
Outputs:
- log_probs: float32 [128, 1024], P('dim', 'corpus')
Inputs may be any that keep to these rules, and one draw needn't show every extreme that they name: `queries`: query rows have real entries of moderate size; their norms differ from row to row. `corpus`: corpus rows have real entries of moderate size; their norms differ from row to row.
All inputs are finite; a program needn't handle non-finite values.
Results may differ from a plain program's by a relative error of at most 0.00095.
Values may be sent and summed in bfloat16 or wider, within the bound.
A program may use at most 64 MiB of HBM per device.

v0:
```python
import jax
import jax.numpy as jnp
from jax import lax
from jax.sharding import PartitionSpec as P


def merged(value, axis, join):
    pieces = jax.tree.map(lambda part: lax.all_gather(part, axis), value)
    head = jax.tree.map(lambda part: part[0], pieces)
    tail = jax.tree.map(lambda part: part[1:], pieces)
    so_far, _ = lax.scan(lambda so_far, section: (join(so_far, section), None), head, tail)
    return so_far


def combine_pair(first, second):
    peak = jnp.maximum(first[0], second[0])
    mass = first[1] * jnp.exp(first[0] - peak) + second[1] * jnp.exp(second[0] - peak)
    return (peak, mass)


def local_pair(scores):
    peak = jnp.max(scores, axis=1)
    mass = jnp.sum(jnp.exp(scores - peak[:, None]), axis=1)
    return (peak, mass)


def pick_owned(scores, indices, offset):
    height = scores.shape[0]
    count = scores.shape[1]
    width = indices.shape[1]
    local = indices - offset
    inside = (local >= 0) & (local < count)
    upper = scores.astype(jnp.bfloat16)
    remain = scores - upper.astype(jnp.float32)
    middle = remain.astype(jnp.bfloat16)
    lower = (remain - middle.astype(jnp.float32)).astype(jnp.bfloat16)
    pieces = jnp.stack([upper, middle, lower], axis=1)
    group = 8

    def select_block(packed):
        block_pieces, block_local = packed
        positions = lax.broadcasted_iota(jnp.int32, (1, 1, count), 2)
        onehot = (block_local[:, :, None] == positions).astype(jnp.bfloat16)
        return jnp.einsum("qkr,qcr->qck", onehot, block_pieces, preferred_element_type=jnp.float32)

    selected = lax.map(
        select_block,
        (
            pieces.reshape(height // group, group, 3, count),
            local.reshape(height // group, group, width),
        ),
    )
    selected = selected.reshape(height, 3, width)
    values = selected[:, 2, :] + selected[:, 1, :] + selected[:, 0, :]
    return jnp.where(inside, values, jnp.float32(0.0))


def body(queries, corpus, candidates):
    rows = corpus.shape[0]
    scores = lax.dot_general(
        queries,
        lax.all_gather(corpus, "dim", axis=1, tiled=True),
        (((1,), (1,)), ((), ())),
        preferred_element_type=jnp.float32,
    )
    peak, mass = merged(local_pair(scores), "corpus", combine_pair)
    own_lse = peak + jnp.log(mass)
    offset = lax.axis_index("corpus") * rows
    picked = pick_owned(scores, candidates, offset)
    logits = lax.psum_scatter(picked, "corpus", scatter_dimension=1, tiled=True)
    return logits - own_lse[:, None]


def solution(mesh):
    placed = (P("dim", None), P("corpus", "dim"), P("dim", None))
    return jax.shard_map(
        body, mesh=mesh, in_specs=placed, out_specs=P("dim", "corpus"), check_vma=False
    )
```

profile of v0, /device:TPU:0, one launch (start us, length us, event | category | flops | bytes accessed | tf_op | source)
XLA Modules:
  0.0 130.3 jit_solution(3010077180744184527)
XLA Ops:
  6.5 2.8 %all_gather.15 = bf16[512,768]{1,0:T(8,128)(2,1)S(1)} all-gather(bf16[512,384]{1,0:T(8,128)(2,1)} %param.8), channel_id=1, replica_groups=mesh['corpus'=16,'dim'=2] {'dim'}, dimensions={1}, use_global_device_ids=true | all-gather | bytes 1179648 | tf_op jit(solution)/shard_map/all_gather | solution.py:62
  9.4 0.4 fusion.17
  9.8 0.2 exponential_reduce_fusion
  10.0 0.1 copy.10
  10.1 0.1 copy.8
  10.4 0.5 pad_maximum_fusion
  10.9 29.6 %while.22 = (s32[]{:T(128)}, f32[8,8,3,1024]{3,1,0,2:T(8,128)S(1)}, bf16[8,8,3,512]{3,2,1,0:T(4,128)(2,1)S(1)}, s32[8,8,1024]{2,1,0:T(8,128)S(1)}, s32[]{:T(128)}) while((s32[]{:T(128)}, f32[8,8,3,1024]{3,1,0,2:T(8,128)S(1)}, bf16[8,8,3,512]{3,2,1,0:T(4,128)(2,1)S(1)}, s32[8,8,1024]{2,1,0:T(8,128)S(1)}, s32[]{:T(128)}) %tuple.38), condition=%wide.region_1.0_spmd, body=%wide.region_0.0_spmd.sunk | while | flops 29360128 | bytes 458825 | solution.py:46
  10.9 3.6 %fusion.24 = f32[1,8,3,1024]{3,2,1,0:T(4,128)S(1)} fusion(s32[8,1024]{1,0:T(8,128)S(1)} %dynamic-slice_bitcast_fusion.2, bf16[8,8,3,512]{3,2,1,0:T(4,128)(2,1)S(1)} %get-tuple-element.158, s32[]{:T(128)} %get-tuple-element.151), kind=kOutput, calls=%fused_computation.3.clone.1 | convolution fusion | flops 29360128 | bytes 163844 | tf_op jit(solution)/shard_map/while/body/eval_jaxpr/qkr,qcr->qck/dot_general | solution.py:44
  14.6 3.6 %fusion.24 = f32[1,8,3,1024]{3,2,1,0:T(4,128)S(1)} fusion(s32[8,1024]{1,0:T(8,128)S(1)} %dynamic-slice_bitcast_fusion.2, bf16[8,8,3,512]{3,2,1,0:T(4,128)(2,1)S(1)} %get-tuple-element.158, s32[]{:T(128)} %get-tuple-element.151), kind=kOutput, calls=%fused_computation.3.clone.1 | convolution fusion | flops 29360128 | bytes 163844 | tf_op jit(solution)/shard_map/while/body/eval_jaxpr/qkr,qcr->qck/dot_general | solution.py:44
  18.3 3.6 %fusion.24 = f32[1,8,3,1024]{3,2,1,0:T(4,128)S(1)} fusion(s32[8,1024]{1,0:T(8,128)S(1)} %dynamic-slice_bitcast_fusion.2, bf16[8,8,3,512]{3,2,1,0:T(4,128)(2,1)S(1)} %get-tuple-element.158, s32[]{:T(128)} %get-tuple-element.151), kind=kOutput, calls=%fused_computation.3.clone.1 | convolution fusion | flops 29360128 | bytes 163844 | tf_op jit(solution)/shard_map/while/body/eval_jaxpr/qkr,qcr->qck/dot_general | solution.py:44
  22.0 3.6 %fusion.24 = f32[1,8,3,1024]{3,2,1,0:T(4,128)S(1)} fusion(s32[8,1024]{1,0:T(8,128)S(1)} %dynamic-slice_bitcast_fusion.2, bf16[8,8,3,512]{3,2,1,0:T(4,128)(2,1)S(1)} %get-tuple-element.158, s32[]{:T(128)} %get-tuple-element.151), kind=kOutput, calls=%fused_computation.3.clone.1 | convolution fusion | flops 29360128 | bytes 163844 | tf_op jit(solution)/shard_map/while/body/eval_jaxpr/qkr,qcr->qck/dot_general | solution.py:44
  25.7 3.6 %fusion.24 = f32[1,8,3,1024]{3,2,1,0:T(4,128)S(1)} fusion(s32[8,1024]{1,0:T(8,128)S(1)} %dynamic-slice_bitcast_fusion.2, bf16[8,8,3,512]{3,2,1,0:T(4,128)(2,1)S(1)} %get-tuple-element.158, s32[]{:T(128)} %get-tuple-element.151), kind=kOutput, calls=%fused_computation.3.clone.1 | convolution fusion | flops 29360128 | bytes 163844 | tf_op jit(solution)/shard_map/while/body/eval_jaxpr/qkr,qcr->qck/dot_general | solution.py:44
  29.4 3.6 %fusion.24 = f32[1,8,3,1024]{3,2,1,0:T(4,128)S(1)} fusion(s32[8,1024]{1,0:T(8,128)S(1)} %dynamic-slice_bitcast_fusion.2, bf16[8,8,3,512]{3,2,1,0:T(4,128)(2,1)S(1)} %get-tuple-element.158, s32[]{:T(128)} %get-tuple-element.151), kind=kOutput, calls=%fused_computation.3.clone.1 | convolution fusion | flops 29360128 | bytes 163844 | tf_op jit(solution)/shard_map/while/body/eval_jaxpr/qkr,qcr->qck/dot_general | solution.py:44
  33.1 3.6 %fusion.24 = f32[1,8,3,1024]{3,2,1,0:T(4,128)S(1)} fusion(s32[8,1024]{1,0:T(8,128)S(1)} %dynamic-slice_bitcast_fusion.2, bf16[8,8,3,512]{3,2,1,0:T(4,128)(2,1)S(1)} %get-tuple-element.158, s32[]{:T(128)} %get-tuple-element.151), kind=kOutput, calls=%fused_computation.3.clone.1 | convolution fusion | flops 29360128 | bytes 163844 | tf_op jit(solution)/shard_map/while/body/eval_jaxpr/qkr,qcr->qck/dot_general | solution.py:44
  36.8 3.6 %fusion.24 = f32[1,8,3,1024]{3,2,1,0:T(4,128)S(1)} fusion(s32[8,1024]{1,0:T(8,128)S(1)} %dynamic-slice_bitcast_fusion.2, bf16[8,8,3,512]{3,2,1,0:T(4,128)(2,1)S(1)} %get-tuple-element.158, s32[]{:T(128)} %get-tuple-element.151), kind=kOutput, calls=%fused_computation.3.clone.1 | convolution fusion | flops 29360128 | bytes 163844 | tf_op jit(solution)/shard_map/while/body/eval_jaxpr/qkr,qcr->qck/dot_general | solution.py:44
  40.6 1.0 copy.12
  41.6 0.6 dynamic-slice
  42.8 0.2 dynamic-update-slice
  43.1 0.2 dynamic-update-slice.1
  43.3 43.9 %all-reduce.2 = (f32[1024]{0:T(1024)S(1)}, f32[1024]{0:T(1024)S(1)}) all-reduce(f32[1024]{0:T(1024)S(1)} %dynamic-update-slice, f32[1024]{0:T(1024)S(1)} %dynamic-update-slice.1), channel_id=2, replica_groups=mesh['corpus'=16,'dim'=2] {'corpus'}, use_global_device_ids=true, to_apply=%add | all-reduce | flops 2048 | bytes 16384
  87.5 0.6 while.23
  88.1 33.8 %reduce-scatter.4.cloned.1.call-done = f32[64,64]{1,0:T(8,128)} async-done(((f32[1024,64]{1,0:T(8,128)}), f32[64,64]{1,0:T(8,128)}) %reduce-scatter.4.cloned.1.call-update) | async-done | bytes 16400
  121.9 0.8 copy.13
  122.7 0.7 broadcast_subtract_fusion
  (52 shorter events, 1.6 us)
Async XLA Ops:
  6.5 2.8 %copy-start = (bf16[64,768]{1,0:T(8,128)(2,1)S(1)}, bf16[64,768]{1,0:T(8,128)(2,1)}, u32[]{:S(2)}) copy-start(bf16[64,768]{1,0:T(8,128)(2,1)} %param.7) | copy-start | bytes 294916
  6.5 115.4 %reduce-scatter.4.cloned.1.call-start = ((), (), s32[]{:S(2)}) async-start(), calls=%async_computation.1 | async-start | bytes 557056
  9.4 1.0 copy-start.1
  40.5 1.0 copy-start.2
Sparse Core Ops, SparseCore 0:
  41.7 80.1 reduce-scatter.3
where the time goes:
time: 131 us; the launch traced here: 130 us
  blocking collectives  46.7 us (36%)
  waiting for transfers between devices  33.8 us (26%)
  matrix products  29.2 us (22%)
  between operations  14.1 us (11%)
  local copies, waits for them, and re-layouts  4.13 us (3%)
  other arithmetic  1.89 us (1%)
    unnamed x1, blocking collectives  43.9 us
    unnamed x2, waiting for transfers between devices  33.8 us
    dot_general x8, matrix products, select_block(): jnp.einsum('qkr,qcr->qck', onehot, block_pieces, preferred_element_type=j...  28.7 us
    unnamed x13, local copies, waits for them, and re-layouts  2.91 us
    all_gather x1, blocking collectives, body(): lax.all_gather(corpus, 'dim', axis=1, tiled=True)  2.82 us
  transfers between devices with their start and end apart: 1, of which 1 were waited for; matrix products, arithmetic and copies ran while one was open for 1% of the time, Pallas kernels for 0%

commit v1 on v0

--- a/solution.py
+++ b/solution.py
@@ -1,7 +1,13 @@
+import functools
 import jax
 import jax.numpy as jnp
 from jax import lax
+from jax.experimental import pallas as pl
+from jax.experimental.pallas import tpu as pltpu
 from jax.sharding import PartitionSpec as P
+
+LANES = 128
+MESH = pl.DeviceIdType.MESH
 
 
 def merged(value, axis, join):
@@ -55,7 +61,7 @@
     return jnp.where(inside, values, jnp.float32(0.0))
 
 
-def body(queries, corpus, candidates):
+def plain_body(queries, corpus, candidates):
     rows = corpus.shape[0]
     scores = lax.dot_general(
         queries,
@@ -71,8 +77,219 @@
     return logits - own_lse[:, None]
 
 
+def times(left, right):
+    return lax.dot_general(
+        left, right, (((1,), (1,)), ((), ())), preferred_element_type=jnp.float32
+    )
+
+
+def kernel(
+    n, q_hbm, c_hbm, k_hbm, out_ref,
+    q, own, other, cand, scores, tiles, got, stat, stats,
+    load_sem, x_send, x_recv, t_send, t_recv, s_send, s_recv,
+):
+    me = lax.axis_index("corpus")
+    side = lax.axis_index("dim")
+    height = q.shape[0]
+    rows, feats = own.shape
+    width = cand.shape[1] // n
+    parts = rows // LANES
+    groups = cand.shape[1] // LANES
+    half = height // 2
+
+    barrier = pltpu.get_barrier_semaphore()
+    pl.semaphore_signal(barrier, inc=1, device_id={"dim": 1 - side}, device_id_type=MESH)
+    for step in range(1, n):
+        pl.semaphore_signal(
+            barrier, inc=1, device_id={"corpus": lax.rem(me + step, n)}, device_id_type=MESH
+        )
+
+    def block(b):
+        return pl.ds(b * LANES, LANES)
+
+    load_q = pltpu.make_async_copy(q_hbm, q, load_sem.at[0])
+    load_k = pltpu.make_async_copy(k_hbm, cand, load_sem.at[1])
+    load_c = [
+        pltpu.make_async_copy(c_hbm.at[block(b)], own.at[block(b)], load_sem.at[2 + b])
+        for b in range(parts)
+    ]
+    load_q.start()
+    for load in load_c:
+        load.start()
+    load_k.start()
+    swaps = [
+        pltpu.make_async_remote_copy(
+            src_ref=own.at[block(b)],
+            dst_ref=other.at[block(b)],
+            send_sem=x_send.at[b],
+            recv_sem=x_recv.at[b],
+            device_id={"dim": 1 - side},
+            device_id_type=MESH,
+        )
+        for b in range(parts)
+    ]
+
+    load_q.wait()
+    q_own = q[:, pl.ds(pl.multiple_of(side * feats, LANES), feats)]
+    for b in range(parts):
+        load_c[b].wait()
+        scores[:, block(b)] = times(q_own, own[block(b), :])
+
+    pl.semaphore_wait(barrier, n)
+    for b in range(parts):
+        swaps[b].start()
+    load_k.wait()
+    q_other = q[:, pl.ds(pl.multiple_of((1 - side) * feats, LANES), feats)]
+    for b in range(parts):
+        swaps[b].wait_recv()
+        scores[:, block(b)] += times(q_other, other[block(b), :])
+
+    def tile_to(p):
+        return pltpu.make_async_remote_copy(
+            src_ref=tiles.at[p],
+            dst_ref=got.at[me],
+            send_sem=t_send.at[p],
+            recv_sem=t_recv.at[me],
+            device_id={"corpus": p},
+            device_id_type=MESH,
+        )
+
+    first = lax.broadcasted_iota(jnp.int32, (half, LANES), 1) < width
+    sends = []
+    ready = []
+    for step in range(groups):
+        away = (step + groups // 2) % groups
+        j = lax.rem(me // 2 + away, groups)
+        local = cand[:, pl.ds(pl.multiple_of(j * LANES, LANES), LANES)] - me * rows
+        lane = local & (LANES - 1)
+        part = lax.shift_right_arithmetic(local, LANES.bit_length() - 1)
+        picked = jnp.zeros((height, LANES), jnp.float32)
+        for b in range(parts):
+            found = jnp.take_along_axis(
+                scores[:, block(b)], lane, axis=1, mode="promise_in_bounds"
+            )
+            picked = jnp.where(part == b, found, picked)
+        low, high = picked[:half], picked[half:]
+        tiles[2 * j] = jnp.where(first, low, pltpu.roll(high, width, 1)).astype(tiles.dtype)
+        tiles[2 * j + 1] = jnp.where(first, pltpu.roll(low, width, 1), high).astype(tiles.dtype)
+        for copy in ready:
+            copy.start()
+        sends += ready
+        if away:
+            ready = [tile_to(2 * j), tile_to(2 * j + 1)]
+        else:
+            ready = [tile_to(2 * j + 1 - lax.rem(me, 2))]
+
+    peak = jnp.max(scores[...], axis=1, keepdims=True)
+    mass = jnp.sum(jnp.exp(scores[...] - peak), axis=1, keepdims=True)
+    lse = peak + jnp.log(mass)
+    for copy in ready:
+        copy.start()
+    sends += ready
+    square = lax.broadcasted_iota(jnp.int32, (height, LANES), 0) == lax.broadcasted_iota(
+        jnp.int32, (height, LANES), 1
+    )
+    stat[...] = jnp.sum(jnp.where(square, lse, 0.0), axis=0, keepdims=True)
+    for step in range(1, n):
+        p = lax.rem(me + step, n)
+        copy = pltpu.make_async_remote_copy(
+            src_ref=stat,
+            dst_ref=stats.at[me],
+            send_sem=s_send.at[p],
+            recv_sem=s_recv.at[me],
+            device_id={"corpus": p},
+            device_id_type=MESH,
+        )
+        copy.start()
+        sends.append(copy)
+
+    total = tiles[me].astype(jnp.float32)
+    lines = [stat[...]]
+    for step in range(1, n):
+        p = lax.rem(me + step, n)
+        pltpu.make_async_remote_copy(
+            src_ref=tiles.at[p],
+            dst_ref=got.at[p],
+            send_sem=t_send.at[p],
+            recv_sem=t_recv.at[p],
+            device_id={"corpus": p},
+            device_id_type=MESH,
+        ).wait_recv()
+        total += got[p].astype(jnp.float32)
+    for step in range(1, n):
+        p = lax.rem(me + step, n)
+        pltpu.make_async_remote_copy(
+            src_ref=stat,
+            dst_ref=stats.at[p],
+            send_sem=s_send.at[p],
+            recv_sem=s_recv.at[p],
+            device_id={"corpus": p},
+            device_id_type=MESH,
+        ).wait_recv()
+        lines.append(stats[p])
+    top = functools.reduce(jnp.maximum, lines)
+    line = top + jnp.log(sum(jnp.exp(item - top) for item in lines))
+    column = jnp.sum(jnp.where(square, line, 0.0), axis=1, keepdims=True)
+    result = total - jnp.where(first, column[:half], column[half:])
+    out_ref[pl.ds(0, half), :] = result[:, :width]
+    out_ref[pl.ds(half, half), :] = pltpu.roll(result, width, 1)[:, :width]
+
+    for copy in swaps + sends:
+        copy.wait_send()
+
+
+def fused_body(n, queries, corpus, candidates):
+    height, depth = queries.shape
+    rows, feats = corpus.shape
+    count = candidates.shape[1]
+    parts = rows // LANES
+    width = count // n
+    dma = pltpu.SemaphoreType.DMA
+    return pl.pallas_call(
+        functools.partial(kernel, n),
+        out_shape=jax.ShapeDtypeStruct((height, width), jnp.float32),
+        in_specs=[pl.BlockSpec(memory_space=pl.ANY)] * 3,
+        out_specs=pl.BlockSpec(memory_space=pltpu.VMEM),
+        scratch_shapes=[
+            pltpu.VMEM((height, depth), queries.dtype),
+            pltpu.VMEM((rows, feats), corpus.dtype),
+            pltpu.VMEM((rows, feats), corpus.dtype),
+            pltpu.VMEM((height, count), jnp.int32),
+            pltpu.VMEM((height, rows), jnp.float32),
+            pltpu.VMEM((n, height // 2, LANES), jnp.bfloat16),
+            pltpu.VMEM((n, height // 2, LANES), jnp.bfloat16),
+            pltpu.VMEM((1, LANES), jnp.float32),
+            pltpu.VMEM((n, 1, LANES), jnp.float32),
+            dma((2 + parts,)),
+            dma((parts,)),
+            dma((parts,)),
+            dma((n,)),
+            dma((n,)),
+            dma((n,)),
+            dma((n,)),
+        ],
+        compiler_params=pltpu.CompilerParams(collective_id=0, has_side_effects=True),
+    )(queries, corpus, candidates)
+
+
+def body(n, cores, queries, corpus, candidates):
+    dense = (
+        cores == 2
+        and candidates.shape[1] == n * LANES // 2
+        and n % 2 == 0
+        and queries.shape[0] <= LANES
+        and queries.shape[0] % 32 == 0
+        and corpus.shape[0] % LANES == 0
+        and corpus.shape[1] % LANES == 0
+    )
+    if dense:
+        return fused_body(n, queries, corpus, candidates)
+    return plain_body(queries, corpus, candidates)
+
+
 def solution(mesh):
     placed = (P("dim", None), P("corpus", "dim"), P("dim", None))
+    sized = functools.partial(body, mesh.shape["corpus"], mesh.shape["dim"])
     return jax.shard_map(
-        body, mesh=mesh, in_specs=placed, out_specs=P("dim", "corpus"), check_vma=False
-    )
+        sized, mesh=mesh, in_specs=placed, out_specs=P("dim", "corpus"), check_vma=False
+    )

time: 131 us -> 16.9 us (0.13)
  blocking collectives: 46.7 us -> 0 us
  waiting for transfers between devices: 33.8 us -> 0 us
  matrix products: 29.2 us -> 0 us
  Pallas kernels: 0 us -> 15.3 us
  between operations: 14.1 us -> 0.01 us
  local copies, waits for them, and re-layouts: 4.13 us -> 1.38 us
  other arithmetic: 1.89 us -> 0 us
    unnamed x1 -> x0, blocking collectives: 43.9 us -> none
    unnamed x2 -> x0, waiting for transfers between devices: 33.8 us -> none
    dot_general x9 -> x0, matrix products: 29.2 us -> none  [the longest x8 28.7 us: select_block(): jnp.einsum('qkr,qcr->qck', onehot, block_pieces, preferred_element_type=j...]
    pallas_call x0 -> x1, Pallas kernels: none -> 15.3 us  [fused_body(): pl.pallas_call(functools.partial(kernel, n), out_shape=jax.ShapeDtypeStru...]
    all_gather x1 -> x0, blocking collectives: 2.82 us -> none  [body(): lax.all_gather(corpus, 'dim', axis=1, tiled=True)]
    unnamed x13 -> x1, local copies, waits for them, and re-layouts: 2.91 us -> 1.38 us
  transfers between devices with their start and end apart: 1 -> 0, of which waited for: 1 -> 0; matrix products, arithmetic and copies ran while one was open for 1% -> 0% of each run, Pallas kernels for 0% -> 0%
where the time goes in v1:
time: 16.9 us; the launch traced here: 16.7 us
  Pallas kernels  15.3 us (91%)
  local copies, waits for them, and re-layouts  1.38 us (8%)
    pallas_call x1, Pallas kernels, fused_body(): pl.pallas_call(functools.partial(kernel, n), out_shape=jax.ShapeDtypeStru...  15.3 us
    unnamed x1, local copies, waits for them, and re-layouts  1.38 us

profile of v1, /device:TPU:0, one launch (start us, length us, event | category | flops | bytes accessed | tf_op | source)
XLA Modules:
  0.0 16.7 jit_solution(15844187750345637985)
XLA Ops:
  0.0 15.3 %shard_map.37 = f32[64,64]{1,0:T(8,128)} custom-call(bf16[64,768]{1,0:T(8,128)(2,1)} %q_hbm.1, bf16[512,384]{1,0:T(8,128)(2,1)} %c_hbm.1, s32[64,1024]{1,0:T(8,128)} %k_hbm.1), custom_call_target="tpu_custom_call" | custom-call | tf_op jit(solution)/shard_map/pallas_call | solution.py:248
  15.3 1.4 %copy.5 = f32[64,64]{1,0:T(8,128)} copy(f32[64,64]{1,0:T(8,128)} %shard_map.37) | data formatting | bytes 32768

commit v2 on v1

--- a/solution.py
+++ b/solution.py
@@ -86,7 +86,7 @@
 def kernel(
     n, q_hbm, c_hbm, k_hbm, out_ref,
     q, own, other, cand, scores, tiles, got, stat, stats,
-    load_sem, x_send, x_recv, t_send, t_recv, s_send, s_recv,
+    wave, load_sem, x_send, x_recv, t_send, t_recv, s_send, s_recv,
 ):
     me = lax.axis_index("corpus")
     side = lax.axis_index("dim")
@@ -97,11 +97,15 @@
     groups = cand.shape[1] // LANES
     half = height // 2
 
+    def across(bit):
+        return me + bit - 2 * bit * lax.rem(me // bit, 2)
+
     barrier = pltpu.get_barrier_semaphore()
+    bits = [1 << i for i in range(n.bit_length() - 1)]
     pl.semaphore_signal(barrier, inc=1, device_id={"dim": 1 - side}, device_id_type=MESH)
-    for step in range(1, n):
+    for bit in bits:
         pl.semaphore_signal(
-            barrier, inc=1, device_id={"corpus": lax.rem(me + step, n)}, device_id_type=MESH
+            barrier, inc=1, device_id={"corpus": across(bit)}, device_id_type=MESH
         )
 
     def block(b):
@@ -113,9 +117,9 @@
         pltpu.make_async_copy(c_hbm.at[block(b)], own.at[block(b)], load_sem.at[2 + b])
         for b in range(parts)
     ]
-    load_q.start()
     for load in load_c:
         load.start()
+    load_q.start()
     load_k.start()
     swaps = [
         pltpu.make_async_remote_copy(
@@ -129,20 +133,35 @@
         for b in range(parts)
     ]
 
+    def tell(i):
+        pl.semaphore_signal(
+            wave.at[i], inc=1, device_id={"corpus": across(bits[i])}, device_id_type=MESH
+        )
+
+    pl.semaphore_wait(barrier, len(bits) + 1)
+    rounds = len(bits) - 1
+    tell(0)
+    for b in range(parts):
+        load_c[b].wait()
+        swaps[b].start()
     load_q.wait()
     q_own = q[:, pl.ds(pl.multiple_of(side * feats, LANES), feats)]
+    q_other = q[:, pl.ds(pl.multiple_of((1 - side) * feats, LANES), feats)]
     for b in range(parts):
-        load_c[b].wait()
         scores[:, block(b)] = times(q_own, own[block(b), :])
-
-    pl.semaphore_wait(barrier, n)
-    for b in range(parts):
-        swaps[b].start()
+    pl.semaphore_wait(wave.at[0], 1)
+    tell(1)
     load_k.wait()
-    q_other = q[:, pl.ds(pl.multiple_of((1 - side) * feats, LANES), feats)]
     for b in range(parts):
         swaps[b].wait_recv()
         scores[:, block(b)] += times(q_other, other[block(b), :])
+        if b == parts // 2 - 1:
+            pl.semaphore_wait(wave.at[1], 1)
+            tell(2)
+    for i in range(2, rounds):
+        pl.semaphore_wait(wave.at[i], 1)
+        if i + 1 < rounds:
+            tell(i + 1)
 
     def tile_to(p):
         return pltpu.make_async_remote_copy(
@@ -155,8 +174,30 @@
         )
 
     first = lax.broadcasted_iota(jnp.int32, (half, LANES), 1) < width
+    square = lax.broadcasted_iota(jnp.int32, (height, LANES), 0) == lax.broadcasted_iota(
+        jnp.int32, (height, LANES), 1
+    )
     sends = []
     ready = []
+
+    def send_stats():
+        peak = jnp.max(scores[...], axis=1, keepdims=True)
+        mass = jnp.sum(jnp.exp(scores[...] - peak), axis=1, keepdims=True)
+        lse = peak + jnp.log(mass)
+        stat[...] = jnp.sum(jnp.where(square, lse, 0.0), axis=0, keepdims=True)
+        for step in range(1, n):
+            p = lax.rem(me + step, n)
+            copy = pltpu.make_async_remote_copy(
+                src_ref=stat,
+                dst_ref=stats.at[me],
+                send_sem=s_send.at[p],
+                recv_sem=s_recv.at[me],
+                device_id={"corpus": p},
+                device_id_type=MESH,
+            )
+            copy.start()
+            sends.append(copy)
+
     for step in range(groups):
         away = (step + groups // 2) % groups
         j = lax.rem(me // 2 + away, groups)
@@ -175,33 +216,16 @@
         for copy in ready:
             copy.start()
         sends += ready
+        if step == groups // 2:
+            send_stats()
         if away:
             ready = [tile_to(2 * j), tile_to(2 * j + 1)]
         else:
             ready = [tile_to(2 * j + 1 - lax.rem(me, 2))]
 
-    peak = jnp.max(scores[...], axis=1, keepdims=True)
-    mass = jnp.sum(jnp.exp(scores[...] - peak), axis=1, keepdims=True)
-    lse = peak + jnp.log(mass)
     for copy in ready:
         copy.start()
     sends += ready
-    square = lax.broadcasted_iota(jnp.int32, (height, LANES), 0) == lax.broadcasted_iota(
-        jnp.int32, (height, LANES), 1
-    )
-    stat[...] = jnp.sum(jnp.where(square, lse, 0.0), axis=0, keepdims=True)
-    for step in range(1, n):
-        p = lax.rem(me + step, n)
-        copy = pltpu.make_async_remote_copy(
-            src_ref=stat,
-            dst_ref=stats.at[me],
-            send_sem=s_send.at[p],
-            recv_sem=s_recv.at[me],
-            device_id={"corpus": p},
-            device_id_type=MESH,
-        )
-        copy.start()
-        sends.append(copy)
 
     total = tiles[me].astype(jnp.float32)
     lines = [stat[...]]
@@ -248,7 +272,7 @@
     return pl.pallas_call(
         functools.partial(kernel, n),
         out_shape=jax.ShapeDtypeStruct((height, width), jnp.float32),
-        in_specs=[pl.BlockSpec(memory_space=pl.ANY)] * 3,
+        in_specs=[pl.BlockSpec(memory_space=pltpu.HBM)] * 3,
         out_specs=pl.BlockSpec(memory_space=pltpu.VMEM),
         scratch_shapes=[
             pltpu.VMEM((height, depth), queries.dtype),
@@ -260,6 +284,7 @@
             pltpu.VMEM((n, height // 2, LANES), jnp.bfloat16),
             pltpu.VMEM((1, LANES), jnp.float32),
             pltpu.VMEM((n, 1, LANES), jnp.float32),
+            pltpu.SemaphoreType.REGULAR((n.bit_length() - 2,)),
             dma((2 + parts,)),
             dma((parts,)),
             dma((parts,)),
@@ -276,7 +301,8 @@
     dense = (
         cores == 2
         and candidates.shape[1] == n * LANES // 2
-        and n % 2 == 0
+        and n >= 16
+        and n & (n - 1) == 0
         and queries.shape[0] <= LANES
         and queries.shape[0] % 32 == 0
         and corpus.shape[0] % LANES == 0

time: 16.9 us -> 17.1 us (1.012)
  Pallas kernels: 15.3 us -> 15.6 us
    pallas_call x1, Pallas kernels: 15.3 us -> 15.6 us  [fused_body(): pl.pallas_call(functools.partial(kernel, n), out_shape=jax.ShapeDtypeStru...]
where the time goes in v2:
time: 17.1 us; the launch traced here: 17 us
  Pallas kernels  15.6 us (91%)
  local copies, waits for them, and re-layouts  1.38 us (8%)
    pallas_call x1, Pallas kernels, fused_body(): pl.pallas_call(functools.partial(kernel, n), out_shape=jax.ShapeDtypeStru...  15.6 us
    unnamed x1, local copies, waits for them, and re-layouts  1.38 us

profile of v2, /device:TPU:0, one launch (start us, length us, event | category | flops | bytes accessed | tf_op | source)
XLA Modules:
  0.0 17.0 jit_solution(2797809552582181744)
XLA Ops:
  0.0 15.6 %shard_map.37 = f32[64,64]{1,0:T(8,128)} custom-call(bf16[64,768]{1,0:T(8,128)(2,1)} %q_hbm.1, bf16[512,384]{1,0:T(8,128)(2,1)} %c_hbm.1, s32[64,1024]{1,0:T(8,128)} %k_hbm.1), custom_call_target="tpu_custom_call" | custom-call | tf_op jit(solution)/shard_map/pallas_call | solution.py:272
  15.6 1.4 %copy.5 = f32[64,64]{1,0:T(8,128)} copy(f32[64,64]{1,0:T(8,128)} %shard_map.37) | data formatting | bytes 32768

commit v3 on v2

--- a/solution.py
+++ b/solution.py
@@ -7,6 +7,7 @@
 from jax.sharding import PartitionSpec as P
 
 LANES = 128
+ROOM = 55169 << 10
 MESH = pl.DeviceIdType.MESH
 
 
@@ -139,7 +140,6 @@
         )
 
     pl.semaphore_wait(barrier, len(bits) + 1)
-    rounds = len(bits) - 1
     tell(0)
     for b in range(parts):
         load_c[b].wait()
@@ -149,19 +149,13 @@
     q_other = q[:, pl.ds(pl.multiple_of((1 - side) * feats, LANES), feats)]
     for b in range(parts):
         scores[:, block(b)] = times(q_own, own[block(b), :])
-    pl.semaphore_wait(wave.at[0], 1)
-    tell(1)
+    for i in range(1, len(bits) - 1):
+        pl.semaphore_wait(wave.at[i - 1], 1)
+        tell(i)
     load_k.wait()
     for b in range(parts):
         swaps[b].wait_recv()
         scores[:, block(b)] += times(q_other, other[block(b), :])
-        if b == parts // 2 - 1:
-            pl.semaphore_wait(wave.at[1], 1)
-            tell(2)
-    for i in range(2, rounds):
-        pl.semaphore_wait(wave.at[i], 1)
-        if i + 1 < rounds:
-            tell(i + 1)
 
     def tile_to(p):
         return pltpu.make_async_remote_copy(
@@ -213,6 +207,8 @@
         low, high = picked[:half], picked[half:]
         tiles[2 * j] = jnp.where(first, low, pltpu.roll(high, width, 1)).astype(tiles.dtype)
         tiles[2 * j + 1] = jnp.where(first, pltpu.roll(low, width, 1), high).astype(tiles.dtype)
+        if step == 0:
+            pl.semaphore_wait(wave.at[len(bits) - 2], 1)
         for copy in ready:
             copy.start()
         sends += ready
@@ -293,7 +289,9 @@
             dma((n,)),
             dma((n,)),
         ],
-        compiler_params=pltpu.CompilerParams(collective_id=0, has_side_effects=True),
+        compiler_params=pltpu.CompilerParams(
+            collective_id=0, has_side_effects=True, vmem_limit_bytes=ROOM
+        ),
     )(queries, corpus, candidates)
 
 

time: 17.1 us -> 15.7 us (0.918)
  local copies, waits for them, and re-layouts: 1.38 us -> 0.62 us
  Pallas kernels: 15.6 us -> 14.9 us
    unnamed x1, local copies, waits for them, and re-layouts: 1.38 us -> 0.62 us
    pallas_call x1, Pallas kernels: 15.6 us -> 14.9 us  [fused_body(): pl.pallas_call(functools.partial(kernel, n), out_shape=jax.ShapeDtypeStru...]
where the time goes in v3:
time: 15.7 us; the launch traced here: 15.6 us
  Pallas kernels  14.9 us (95%)
  local copies, waits for them, and re-layouts  0.62 us (4%)
    pallas_call x1, Pallas kernels, fused_body(): pl.pallas_call(functools.partial(kernel, n), out_shape=jax.ShapeDtypeStru...  14.9 us
    unnamed x1, local copies, waits for them, and re-layouts  0.62 us

profile of v3, /device:TPU:0, one launch (start us, length us, event | category | flops | bytes accessed | tf_op | source)
XLA Modules:
  0.0 15.6 jit_solution(18285221411934456440)
XLA Ops:
  0.0 14.9 %shard_map.37 = f32[64,64]{1,0:T(8,128)S(1)} custom-call(bf16[64,768]{1,0:T(8,128)(2,1)} %q_hbm.1, bf16[512,384]{1,0:T(8,128)(2,1)} %c_hbm.1, s32[64,1024]{1,0:T(8,128)} %k_hbm.1), custom_call_target="tpu_custom_call" | custom-call | tf_op jit(solution)/shard_map/pallas_call | solution.py:268
  14.9 0.6 %copy.5 = f32[64,64]{1,0:T(8,128)} copy(f32[64,64]{1,0:T(8,128)S(1)} %shard_map.37) | data formatting | bytes 32768

commit v4 on v3

--- a/solution.py
+++ b/solution.py
@@ -98,16 +98,24 @@
     groups = cand.shape[1] // LANES
     half = height // 2
 
-    def across(bit):
-        return me + bit - 2 * bit * lax.rem(me // bit, 2)
+    def flipped(value, mask):
+        for i in range(mask.bit_length()):
+            bit = 1 << i
+            if mask & bit:
+                value = value + bit - 2 * bit * lax.rem(value // bit, 2)
+        return value
 
     barrier = pltpu.get_barrier_semaphore()
-    bits = [1 << i for i in range(n.bit_length() - 1)]
-    pl.semaphore_signal(barrier, inc=1, device_id={"dim": 1 - side}, device_id_type=MESH)
-    for bit in bits:
+    partner_in, all_in = wave.at[0], wave.at[1]
+
+    def tell_partner(semaphore):
         pl.semaphore_signal(
-            barrier, inc=1, device_id={"corpus": across(bit)}, device_id_type=MESH
+            semaphore, inc=1, device_id={"dim": 1 - side}, device_id_type=MESH
         )
+
+    @pl.when(side == 0)
+    def _():
+        tell_partner(barrier)
 
     def block(b):
         return pl.ds(b * LANES, LANES)
@@ -134,13 +142,19 @@
         for b in range(parts)
     ]
 
-    def tell(i):
-        pl.semaphore_signal(
-            wave.at[i], inc=1, device_id={"corpus": across(bits[i])}, device_id_type=MESH
-        )
-
-    pl.semaphore_wait(barrier, len(bits) + 1)
-    tell(0)
+    @pl.when(side == 1)
+    def _():
+        pl.semaphore_wait(barrier, 1)
+        tell_partner(partner_in)
+
+    @pl.when(side == 0)
+    def _():
+        pl.semaphore_wait(partner_in, 1)
+        for step in range(1, n):
+            pl.semaphore_signal(
+                barrier, inc=1, device_id={"corpus": lax.rem(me + step, n)}, device_id_type=MESH
+            )
+
     for b in range(parts):
         load_c[b].wait()
         swaps[b].start()
@@ -149,13 +163,20 @@
     q_other = q[:, pl.ds(pl.multiple_of((1 - side) * feats, LANES), feats)]
     for b in range(parts):
         scores[:, block(b)] = times(q_own, own[block(b), :])
-    for i in range(1, len(bits) - 1):
-        pl.semaphore_wait(wave.at[i - 1], 1)
-        tell(i)
     load_k.wait()
     for b in range(parts):
         swaps[b].wait_recv()
         scores[:, block(b)] += times(q_other, other[block(b), :])
+
+    def wait_for_all():
+        @pl.when(side == 0)
+        def _():
+            pl.semaphore_wait(barrier, n - 1)
+            tell_partner(all_in)
+
+        @pl.when(side == 1)
+        def _():
+            pl.semaphore_wait(all_in, 1)
 
     def tile_to(p):
         return pltpu.make_async_remote_copy(
@@ -193,8 +214,8 @@
             sends.append(copy)
 
     for step in range(groups):
-        away = (step + groups // 2) % groups
-        j = lax.rem(me // 2 + away, groups)
+        away = groups - 1 - step
+        j = flipped(me // 2, away)
         local = cand[:, pl.ds(pl.multiple_of(j * LANES, LANES), LANES)] - me * rows
         lane = local & (LANES - 1)
         part = lax.shift_right_arithmetic(local, LANES.bit_length() - 1)
@@ -208,7 +229,7 @@
         tiles[2 * j] = jnp.where(first, low, pltpu.roll(high, width, 1)).astype(tiles.dtype)
         tiles[2 * j + 1] = jnp.where(first, pltpu.roll(low, width, 1), high).astype(tiles.dtype)
         if step == 0:
-            pl.semaphore_wait(wave.at[len(bits) - 2], 1)
+            wait_for_all()
         for copy in ready:
             copy.start()
         sends += ready
@@ -223,19 +244,7 @@
         copy.start()
     sends += ready
 
-    total = tiles[me].astype(jnp.float32)
     lines = [stat[...]]
-    for step in range(1, n):
-        p = lax.rem(me + step, n)
-        pltpu.make_async_remote_copy(
-            src_ref=tiles.at[p],
-            dst_ref=got.at[p],
-            send_sem=t_send.at[p],
-            recv_sem=t_recv.at[p],
-            device_id={"corpus": p},
-            device_id_type=MESH,
-        ).wait_recv()
-        total += got[p].astype(jnp.float32)
     for step in range(1, n):
         p = lax.rem(me + step, n)
         pltpu.make_async_remote_copy(
@@ -250,6 +259,18 @@
     top = functools.reduce(jnp.maximum, lines)
     line = top + jnp.log(sum(jnp.exp(item - top) for item in lines))
     column = jnp.sum(jnp.where(square, line, 0.0), axis=1, keepdims=True)
+    total = tiles[me].astype(jnp.float32)
+    for step in range(1, n):
+        p = lax.rem(me + step, n)
+        pltpu.make_async_remote_copy(
+            src_ref=tiles.at[p],
+            dst_ref=got.at[p],
+            send_sem=t_send.at[p],
+            recv_sem=t_recv.at[p],
+            device_id={"corpus": p},
+            device_id_type=MESH,
+        ).wait_recv()
+        total += got[p].astype(jnp.float32)
     result = total - jnp.where(first, column[:half], column[half:])
     out_ref[pl.ds(0, half), :] = result[:, :width]
     out_ref[pl.ds(half, half), :] = pltpu.roll(result, width, 1)[:, :width]
@@ -280,7 +301,7 @@
             pltpu.VMEM((n, height // 2, LANES), jnp.bfloat16),
             pltpu.VMEM((1, LANES), jnp.float32),
             pltpu.VMEM((n, 1, LANES), jnp.float32),
-            pltpu.SemaphoreType.REGULAR((n.bit_length() - 2,)),
+            pltpu.SemaphoreType.REGULAR((2,)),
             dma((2 + parts,)),
             dma((parts,)),
             dma((parts,)),

time: 15.7 us -> 14.8 us (0.943)
  Pallas kernels: 14.9 us -> 14 us
    pallas_call x1, Pallas kernels: 14.9 us -> 14 us  [fused_body(): pl.pallas_call(functools.partial(kernel, n), out_shape=jax.ShapeDtypeStru...]
where the time goes in v4:
time: 14.8 us; the launch traced here: 14.6 us
  Pallas kernels  14 us (95%)
  local copies, waits for them, and re-layouts  0.62 us (4%)
    pallas_call x1, Pallas kernels, fused_body(): pl.pallas_call(functools.partial(kernel, n), out_shape=jax.ShapeDtypeStru...  14 us
    unnamed x1, local copies, waits for them, and re-layouts  0.62 us

profile of v4, /device:TPU:0, one launch (start us, length us, event | category | flops | bytes accessed | tf_op | source)
XLA Modules:
  0.0 14.6 jit_solution(15680443185111676365)
XLA Ops:
  0.0 14.0 %shard_map.37 = f32[64,64]{1,0:T(8,128)S(1)} custom-call(bf16[64,768]{1,0:T(8,128)(2,1)} %q_hbm.1, bf16[512,384]{1,0:T(8,128)(2,1)} %c_hbm.1, s32[64,1024]{1,0:T(8,128)} %k_hbm.1), custom_call_target="tpu_custom_call" | custom-call | tf_op jit(solution)/shard_map/pallas_call | solution.py:289
  14.0 0.6 %copy.5 = f32[64,64]{1,0:T(8,128)} copy(f32[64,64]{1,0:T(8,128)S(1)} %shard_map.37) | data formatting | bytes 32768

commit v5 on v4

--- a/solution.py
+++ b/solution.py
@@ -193,9 +193,9 @@
         jnp.int32, (height, LANES), 1
     )
     sends = []
-    ready = []
-
-    def send_stats():
+    line_sends = []
+
+    def make_stats():
         peak = jnp.max(scores[...], axis=1, keepdims=True)
         mass = jnp.sum(jnp.exp(scores[...] - peak), axis=1, keepdims=True)
         lse = peak + jnp.log(mass)
@@ -210,8 +210,7 @@
                 device_id={"corpus": p},
                 device_id_type=MESH,
             )
-            copy.start()
-            sends.append(copy)
+            line_sends.append(copy)
 
     for step in range(groups):
         away = groups - 1 - step
@@ -228,21 +227,16 @@
         low, high = picked[:half], picked[half:]
         tiles[2 * j] = jnp.where(first, low, pltpu.roll(high, width, 1)).astype(tiles.dtype)
         tiles[2 * j + 1] = jnp.where(first, pltpu.roll(low, width, 1), high).astype(tiles.dtype)
-        if step == 0:
-            wait_for_all()
-        for copy in ready:
-            copy.start()
-        sends += ready
-        if step == groups // 2:
-            send_stats()
         if away:
-            ready = [tile_to(2 * j), tile_to(2 * j + 1)]
+            sends += [tile_to(2 * j), tile_to(2 * j + 1)]
         else:
-            ready = [tile_to(2 * j + 1 - lax.rem(me, 2))]
-
-    for copy in ready:
+            sends += [tile_to(2 * j + 1 - lax.rem(me, 2))]
+
+    make_stats()
+    wait_for_all()
+    sends = sends[: n // 2] + line_sends + sends[n // 2 :]
+    for copy in sends:
         copy.start()
-    sends += ready
 
     lines = [stat[...]]
     for step in range(1, n):

time: 14.8 us -> 14.8 us (level)
  no operation moved by 1% of the time
where the time goes in v5:
time: 14.8 us; the launch traced here: 14.7 us
  Pallas kernels  14 us (95%)
  local copies, waits for them, and re-layouts  0.62 us (4%)
    pallas_call x1, Pallas kernels, fused_body(): pl.pallas_call(functools.partial(kernel, n), out_shape=jax.ShapeDtypeStru...  14 us
    unnamed x1, local copies, waits for them, and re-layouts  0.62 us

profile of v5, /device:TPU:0, one launch (start us, length us, event | category | flops | bytes accessed | tf_op | source)
XLA Modules:
  0.0 14.7 jit_solution(5863043007388494065)
XLA Ops:
  0.0 14.0 %shard_map.37 = f32[64,64]{1,0:T(8,128)S(1)} custom-call(bf16[64,768]{1,0:T(8,128)(2,1)} %q_hbm.1, bf16[512,384]{1,0:T(8,128)(2,1)} %c_hbm.1, s32[64,1024]{1,0:T(8,128)} %k_hbm.1), custom_call_target="tpu_custom_call" | custom-call | tf_op jit(solution)/shard_map/pallas_call | solution.py:283
  14.1 0.6 %copy.5 = f32[64,64]{1,0:T(8,128)} copy(f32[64,64]{1,0:T(8,128)S(1)} %shard_map.37) | data formatting | bytes 32768
